TPU v7x, 32 devices: a whole 2x2x4 slice. The times are simulated.
32 devices in a mesh: segment: 4 (over y, core), dp: 8 (over z, x).
Axes of the slice: x: 2, y: 2, z: 4, core: 2. Of those that a mesh axis runs over, the one named last changes fastest.
Arguments:
- token_ids: int32 [1024], P('dp'), may hold values from 0 to 38015, as said below
- table: bfloat16 [4752, 28672], P('segment', 'dp'), may hold values from -6 to 6
- out_grad: bfloat16 [1024, 3584], P('dp', 'segment'), may hold values from -6 to 6
Outputs:
- embedded: bfloat16 [1024, 3584], P('dp')
- table_grad: bfloat16 [4752, 28672], P('segment', 'dp')
Inputs may be any that keep to these rules, and one draw needn't show every extreme that they name: `token_ids`: in the 128 tokens of each data group, at most 16 ids lie in one segment's slice of 9504 rows with one residue modulo 8; in every data group some segment and residue has exactly 16.
All inputs are finite; a program needn't handle non-finite values.
Results may differ from a plain program's by a relative error of at most 0.001.
Values may be sent and summed in bfloat16 or wider, within the bound.
A program may use at most 64 MiB of HBM per device.

v0:
```python
import jax
import jax.numpy as jnp
from jax import lax
from jax.sharding import PartitionSpec as P

D = 3584
PACK = 8


def body(token_ids, table, out_grad):
    lines = table.shape[0]
    width = table.shape[1]
    groups = lax.axis_size("dp")
    tok_rows = token_ids.shape[0]
    quarters = D // width
    slot = lax.axis_index("dp") // quarters
    first = lax.axis_index("segment") * lines * PACK
    every_id = lax.all_gather(token_ids, "dp", axis=0, tiled=True)
    local = every_id - first
    in_section = (local >= 0) & (local < lines * PACK)
    owned = in_section & (local % PACK == slot)
    line_idx = jnp.clip(local // PACK, 0, lines - 1)
    whole_grad = lax.all_gather(out_grad, "segment", axis=1, tiled=True)
    capacity = tok_rows // PACK
    owned_grid = owned.reshape(groups, tok_rows)
    rank = jnp.cumsum(owned_grid.astype(jnp.int32), axis=1) - 1
    place = jnp.where(owned_grid, rank, capacity)
    group_rows = jnp.broadcast_to(jnp.arange(groups, dtype=jnp.int32)[:, None], (groups, tok_rows))
    row_of = (
        jnp.zeros((groups, capacity), jnp.int32)
        .at[group_rows, place]
        .set(line_idx.reshape(groups, tok_rows), mode="drop")
    )
    filled = jnp.zeros((groups, capacity), jnp.bool_).at[group_rows, place].set(True, mode="drop")
    fetched = jnp.take(table, row_of.reshape(-1), axis=0).reshape(groups, capacity, width)
    fetched = jnp.where(filled[:, :, None], fetched, jnp.zeros((), jnp.bfloat16))
    arrived = lax.all_to_all(fetched, "dp", split_axis=0, concat_axis=0, tiled=True)
    my_local = token_ids - first
    my_in = (my_local >= 0) & (my_local < lines * PACK)
    my_slot = my_local % PACK
    slot_hits = (my_slot[:, None] == jnp.arange(PACK, dtype=jnp.int32)[None, :]) & my_in[:, None]
    slot_ranks = jnp.cumsum(slot_hits.astype(jnp.int32), axis=0) - 1
    my_rank = jnp.sum(jnp.where(slot_hits, slot_ranks, 0), axis=1)
    sources = my_slot[:, None] * quarters + jnp.arange(quarters, dtype=jnp.int32)[None, :]
    flat_index = jnp.clip(sources * capacity + my_rank[:, None], 0, groups * capacity - 1)
    gathered = jnp.take(
        arrived.reshape(groups * capacity, width), flat_index.reshape(-1), axis=0
    ).reshape(tok_rows, D)
    segment_part = jnp.where(my_in[:, None], gathered.astype(jnp.float32), 0.0)
    slot_place = jnp.where(my_in, my_slot, PACK)
    token_at = (
        jnp.zeros((PACK, capacity), jnp.int32)
        .at[slot_place, my_rank]
        .set(jnp.arange(tok_rows, dtype=jnp.int32), mode="drop")
    )
    valid = jnp.zeros((PACK, capacity), jnp.bool_).at[slot_place, my_rank].set(True, mode="drop")
    grad_pick = jnp.take(whole_grad, token_at.reshape(-1), axis=0).reshape(
        PACK, capacity, quarters, width
    )
    grad_pick = jnp.where(valid[:, :, None, None], grad_pick, jnp.zeros((), jnp.bfloat16))
    grad_send = grad_pick.transpose(0, 2, 1, 3).reshape(groups, capacity, width)
    returned = lax.all_to_all(grad_send, "dp", split_axis=0, concat_axis=0, tiled=True)
    target = jnp.where(filled, row_of, lines)
    accum = (
        jnp.zeros((lines, width), jnp.float32)
        .at[target.reshape(-1)]
        .add(returned.reshape(-1, width).astype(jnp.float32), mode="drop")
    )
    embedded = lax.psum(segment_part.astype(jnp.bfloat16), "segment")
    return (embedded, accum.astype(jnp.bfloat16))


def solution(mesh):
    placed = (P("dp"), P("segment", "dp"), P("dp", "segment"))
    return jax.shard_map(
        body,
        mesh=mesh,
        in_specs=placed,
        out_specs=(P("dp", None), P("segment", "dp")),
        check_vma=False,
    )
```

profile of v0, /device:TPU:0, one launch (start us, length us, event | category | flops | bytes accessed | tf_op | source)
XLA Modules:
  0.0 159.1 jit_solution(7434590179938538914)
XLA Ops:
  7.2 22.6 %all-gather = s32[8,1,128]{2,1,0:T(1,128)S(1)} all-gather(s32[1,1,128]{2,1,0:T(1,128)} %bitcast.39), channel_id=1, replica_groups=mesh['segment'=4,'dp'=8] {'dp'}, dimensions={0}, use_global_device_ids=true | all-gather | bytes 4608 | tf_op jit(solution)/shard_map/all_gather | solution.py:18
  29.8 0.3 copy.12
  30.1 0.3 copy.13
  30.4 23.6 %compare_select_fusion = s32[8,128,1]{2,0,1:T(8,128)S(1)} fusion(pred[8,128,1]{2,0,1:T(8,128)(4,1)S(1)} %copy.13, s32[8,128,1]{2,0,1:T(8,128)S(1)} %copy.12), kind=kOutput, calls=%fused_computation.12 | output fusion | flops 135168 | bytes 9216 | tf_op jit(solution)/shard_map/jit(cumsum)/reduce_window_sum | solution.py:26
  54.0 0.2 copy.14
  54.2 0.8 multiply_reduce_fusion
  55.0 0.1 copy.19
  55.1 0.7 and_reduce_fusion
  55.8 0.1 copy.18
  56.0 4.3 %scatter_custom_fusion.4 = s32[128]{0:T(128)S(1)} fusion(s32[1024]{0:T(1024)S(1)} %bitcast.40, s32[1024]{0:T(1024)S(1)} %fusion.6, s32[]{:T(128)} %constant.70.clone.1), kind=kCustom, calls=%fused_computation.66 | custom fusion | bytes 516
  60.4 4.3 %scatter_custom_fusion.3 = pred[128]{0:T(512)(128)(4,1)S(1)} fusion(s32[1024]{0:T(1024)S(1)} %bitcast.41, pred[1024]{0:T(1024)(128)(4,1)S(1)} %broadcast.224, pred[]{:T(512)} %constant.71.clone.1), kind=kCustom, calls=%fused_computation.56 | custom fusion | bytes 129
  64.8 0.1 reshape.185
  64.9 6.6 %gather_fusion = bf16[128,3584]{1,0:T(8,128)(2,1)S(1)} fusion(bf16[1188,3584]{1,0:T(8,128)(2,1)} %param.6, s32[1024]{0:T(1024)S(1)} %pad_clamp_fusion.2), kind=kCustom, calls=%fused_computation.2 | custom fusion | bytes 1835520 | tf_op jit(solution)/shard_map/jit(_take)/gather | solution.py:35
  71.4 1.1 select_select_fusion
  72.6 3.6 %all-to-all-start = ((bf16[8,16,3584]{2,1,0:T(8,128)(2,1)}), bf16[8,16,3584]{2,1,0:T(8,128)(2,1)S(1)}, u32[]{:S(2)}, u32[]{:S(2)}) async-start(bf16[8,16,3584]{2,1,0:T(8,128)(2,1)} %select_select_fusion), calls=%async_computation | async-start | bytes 1835008 | tf_op jit(solution)/shard_map/all_to_all | solution.py:37
  76.2 0.1 fusion.4
  76.3 0.2 reduce_window_sum.23
  76.4 0.2 select_reduce_fusion
  76.7 6.4 %scatter_fusion.1 = s32[8,16]{1,0:T(8,128)S(1)} fusion(s32[8,16]{1,0:T(8,128)S(1)} %broadcast.169, s32[128]{0:T(128)S(1)} %fusion.18, s32[128]{0:T(128)S(1)} %iota.14), kind=kCustom, calls=%fused_computation.4 | custom fusion | bytes 2560 | tf_op jit(solution)/shard_map/scatter | solution.py:54
  83.0 0.1 reshape.180
  83.2 9.5 %all_gather.7 = bf16[128,3584]{1,0:T(8,128)(2,1)S(1)} all-gather(bf16[128,896]{1,0:T(8,128)(2,1)S(1)} %copy-done), channel_id=1, replica_groups=mesh['segment'=4,'dp'=8] {'segment'}, dimensions={1}, use_global_device_ids=true | all-gather | bytes 1146880 | tf_op jit(solution)/shard_map/all_gather | solution.py:23
  92.7 1.1 gather_fusion.2
  93.8 6.5 %scatter_fusion = pred[8,16]{1,0:T(8,128)(4,1)S(1)} fusion(pred[8,16]{1,0:T(8,128)(4,1)S(1)} %broadcast.166, s32[128]{0:T(128)S(1)} %fusion.18, pred[128]{0:T(512)(128)(4,1)S(1)} %broadcast.225), kind=kCustom, calls=%fused_computation.3 | custom fusion | bytes 1408 | tf_op jit(solution)/shard_map/scatter | solution.py:56
  100.3 0.2 broadcast_select_fusion
  100.5 1.1 broadcast_select_fusion.1
  101.5 5.9 %all-to-all-start.1 = ((bf16[8,16,3584]{2,1,0:T(8,128)(2,1)}), bf16[8,16,3584]{2,1,0:T(8,128)(2,1)S(1)}, u32[]{:S(2)}, u32[]{:S(2)}) async-start(bf16[8,16,3584]{2,1,0:T(8,128)(2,1)} %broadcast_select_fusion.1), calls=%async_computation.1 | async-start | bytes 1835008 | tf_op jit(solution)/shard_map/all_to_all | solution.py:62
  107.5 1.1 gather_fusion.1
  108.7 1.3 select_convert_fusion
  110.1 20.9 %all-to-all-done.1 = bf16[8,16,3584]{2,1,0:T(8,128)(2,1)S(1)} async-done(((bf16[8,16,3584]{2,1,0:T(8,128)(2,1)}), bf16[8,16,3584]{2,1,0:T(8,128)(2,1)S(1)}, u32[]{:S(2)}, u32[]{:S(2)}) %all-to-all-start.1) | async-done | bytes 917536 | tf_op jit(solution)/shard_map/all_to_all | solution.py:62
  130.9 10.0 %scatter_custom_fusion.2 = f32[1188,3584]{1,0:T(8,128)} fusion(s32[128]{0:T(128)S(1)} %fusion.16, f32[]{:T(128)} %constant.121.clone.1, bf16[128,3584]{1,0:T(8,128)(2,1)S(1)} %bitcast.35), kind=kCustom, calls=%fused_computation.8 | custom fusion | flops 917504 | bytes 17948676 | tf_op jit(solution)/shard_map/scatter-add | solution.py:67
  140.9 9.1 %convert_element_type.32 = bf16[1188,3584]{1,0:T(8,128)(2,1)} convert(f32[1188,3584]{1,0:T(8,128)} %scatter_custom_fusion.2) | non-fusion elementwise | flops 4257792 | bytes 25546752 | tf_op jit(solution)/shard_map/convert_element_type | solution.py:70
  150.1 2.2 %copy.23 = bf16[128,3584]{1,0:T(8,128)(2,1)} copy(bf16[128,3584]{1,0:T(8,128)(2,1)} %all-reduce.2.cloned.1.call-done) | data formatting | bytes 1835008
  (34 shorter events, 0.5 us)
Async XLA Ops:
  7.2 69.0 %copy-start.1 = (s32[128]{0:T(128)S(1)}, s32[128]{0:T(128)}, u32[]{:S(2)}) copy-start(s32[128]{0:T(128)} %param.5) | copy-start | bytes 1540
  7.2 76.0 %copy-start = (bf16[128,896]{1,0:T(8,128)(2,1)S(1)}, bf16[128,896]{1,0:T(8,128)(2,1)}, u32[]{:S(2)}) copy-start(bf16[128,896]{1,0:T(8,128)(2,1)} %param.7) | copy-start | bytes 688132
  72.6 29.0 %all-to-all-start = ((bf16[8,16,3584]{2,1,0:T(8,128)(2,1)}), bf16[8,16,3584]{2,1,0:T(8,128)(2,1)S(1)}, u32[]{:S(2)}, u32[]{:S(2)}) async-start(bf16[8,16,3584]{2,1,0:T(8,128)(2,1)} %select_select_fusion), calls=%async_computation | async-start | bytes 1835008 | tf_op jit(solution)/shard_map/all_to_all | solution.py:37
  101.5 29.4 %all-to-all-start.1 = ((bf16[8,16,3584]{2,1,0:T(8,128)(2,1)}), bf16[8,16,3584]{2,1,0:T(8,128)(2,1)S(1)}, u32[]{:S(2)}, u32[]{:S(2)}) async-start(bf16[8,16,3584]{2,1,0:T(8,128)(2,1)} %broadcast_select_fusion.1), calls=%async_computation.1 | async-start | bytes 1835008 | tf_op jit(solution)/shard_map/all_to_all | solution.py:62
  107.5 42.6 %all-reduce.2.cloned.1.call-start = ((), (), s32[]{:S(2)}) async-start(), calls=%async_computation.2 | async-start | bytes 1835008 | tf_op jit(solution)/shard_map/psum | solution.py:69
Sparse Core Ops, SparseCore 0:
  111.2 36.2 all-reduce.1
where the time goes:
time: 159 us
  other arithmetic  48.5 us (31%)
  local copies, waits for them, and re-layouts  33.8 us (21%)
  blocking collectives  32.1 us (20%)
  waiting for transfers between devices  20.9 us (13%)
  between operations  14.3 us (9%)
  starting transfers between devices  9.52 us (6%)
    another operation x1, other arithmetic, body(): rank = jnp.cumsum(owned_grid.astype(jnp.int32), axis=1) - 1  23.6 us
    all_gather x1, blocking collectives, body(): every_id = lax.all_gather(token_ids, 'dp', axis=0, tiled=True)  22.6 us
    all_to_all x1, waiting for transfers between devices, body(): lax.all_to_all(grad_send, 'dp', split_axis=0, concat_axis=0, tiled=True)  20.9 us
    unnamed x11, local copies, waits for them, and re-layouts  11.1 us
    scatter-add x1, other arithmetic, body(): accum = jnp.zeros((lines, width), jnp.float32).at[target.reshape(-1)].add...  10 us
    all_gather x1, blocking collectives, body(): whole_grad = lax.all_gather(out_grad, 'segment', axis=1, tiled=True)  9.52 us
    convert_element_type x1, other arithmetic, body(): return (embedded, accum.astype(jnp.bfloat16))  9.14 us
    gather x1, local copies, waits for them, and re-layouts, body(): jnp.take(table, row_of.reshape(-1), axis=0).reshape(groups, capacity, width)  6.55 us
  transfers between devices with their start and end apart: 3, of which 1 were waited for; matrix products, arithmetic and copies ran while one was open for 24% of the time, Pallas kernels for 0%

commit v1 on v0

--- a/solution.py
+++ b/solution.py
@@ -5,6 +5,27 @@
 
 D = 3584
 PACK = 8
+
+
+def open_values_in(buf, which_dim):
+    answer = list(buf.shape[1:])
+    answer[which_dim] *= buf.shape[0]
+    return jnp.moveaxis(buf, 0, which_dim).reshape(answer)
+
+
+def switch_corner(view, group_axis):
+    y1 = lax.axis_size(group_axis)
+    big = lax.axis_index(group_axis)
+    new, wide_out = (y1, big)
+    tall, m_next = (view[None], 1)
+    while m_next < new:
+        u1 = lax.ppermute(tall, group_axis, [(hop_no, hop_no ^ m_next) for hop_no in range(new)])
+        res = wide_out & m_next == 0
+        arr_out = jnp.where(res, tall, u1)
+        q_next = jnp.where(res, u1, tall)
+        tall = jnp.concatenate([arr_out, q_next])
+        m_next *= 2
+    return tall
 
 
 def body(token_ids, table, out_grad):
@@ -20,7 +41,8 @@
     in_section = (local >= 0) & (local < lines * PACK)
     owned = in_section & (local % PACK == slot)
     line_idx = jnp.clip(local // PACK, 0, lines - 1)
-    whole_grad = lax.all_gather(out_grad, "segment", axis=1, tiled=True)
+    met_up = switch_corner(out_grad, "segment")
+    whole_grad = open_values_in(met_up, 1)
     capacity = tok_rows // PACK
     owned_grid = owned.reshape(groups, tok_rows)
     rank = jnp.cumsum(owned_grid.astype(jnp.int32), axis=1) - 1

time: 159 us -> 158 us (level)
  blocking collectives: 32.1 us -> 22 us
  waiting for transfers between devices: 20.9 us -> 26.8 us
  starting transfers between devices: 9.52 us -> 11.4 us
    all_gather x1 -> x0, blocking collectives: 9.52 us -> none  [body(): whole_grad = lax.all_gather(out_grad, 'segment', axis=1, tiled=True)]
    ppermute x0 -> x2, waiting for transfers between devices: none -> 7.61 us  [switch_corner(): lax.ppermute(tall, group_axis, [(hop_no, hop_no ^ m_next) for hop_no in r...]
    all_to_all x1, waiting for transfers between devices: 20.9 us -> 16.3 us  [body(): lax.all_to_all(grad_send, 'dp', split_axis=0, concat_axis=0, tiled=True)]
    psum x1, waiting for transfers between devices: 0.01 us -> 2.81 us  [body(): embedded = lax.psum(segment_part.astype(jnp.bfloat16), 'segment')]
    ppermute x0 -> x2, starting transfers between devices: none -> 2.15 us  [switch_corner(): lax.ppermute(tall, group_axis, [(hop_no, hop_no ^ m_next) for hop_no in r...]
  transfers between devices with their start and end apart: 3 -> 5, of which waited for: 1 -> 3; matrix products, arithmetic and copies ran while one was open for 24% -> 51% of each run, Pallas kernels for 0% -> 0%
where the time goes in v1:
time: 158 us; the launch traced here: 157 us
  other arithmetic  48.9 us (31%)
  local copies, waits for them, and re-layouts  33.9 us (21%)
  waiting for transfers between devices  26.8 us (17%)
  blocking collectives  22 us (14%)
  between operations  14.3 us (9%)
  starting transfers between devices  11.4 us (7%)
    another operation x1, other arithmetic, body(): rank = jnp.cumsum(owned_grid.astype(jnp.int32), axis=1) - 1  23.6 us
    all_gather x1, blocking collectives, body(): every_id = lax.all_gather(token_ids, 'dp', axis=0, tiled=True)  22 us
    all_to_all x1, waiting for transfers between devices, body(): lax.all_to_all(grad_send, 'dp', split_axis=0, concat_axis=0, tiled=True)  16.3 us
    unnamed x11, local copies, waits for them, and re-layouts  11.1 us
    scatter-add x1, other arithmetic, body(): accum = jnp.zeros((lines, width), jnp.float32).at[target.reshape(-1)].add...  9.95 us
    convert_element_type x1, other arithmetic, body(): return (embedded, accum.astype(jnp.bfloat16))  9.27 us
    ppermute x2, waiting for transfers between devices, switch_corner(): lax.ppermute(tall, group_axis, [(hop_no, hop_no ^ m_next) for hop_no in r...  7.61 us
    gather x1, local copies, waits for them, and re-layouts, body(): jnp.take(table, row_of.reshape(-1), axis=0).reshape(groups, capacity, width)  6.55 us
  transfers between devices with their start and end apart: 5, of which 3 were waited for; matrix products, arithmetic and copies ran while one was open for 51% of the time, Pallas kernels for 0%

profile of v1, /device:TPU:0, one launch (start us, length us, event | category | flops | bytes accessed | tf_op | source)
XLA Modules:
  0.0 157.2 jit_solution(17998725026225555937)
XLA Ops:
  7.2 0.6 collective-permute-start
  7.7 22.0 %all-gather = s32[8,1,128]{2,1,0:T(1,128)S(1)} all-gather(s32[1,1,128]{2,1,0:T(1,128)} %bitcast.48), channel_id=1, replica_groups=mesh['segment'=4,'dp'=8] {'dp'}, dimensions={0}, use_global_device_ids=true | all-gather | bytes 4608 | tf_op jit(solution)/shard_map/all_gather | solution.py:39
  29.7 0.3 copy.15
  30.0 0.3 copy.16
  30.3 23.6 %compare_select_fusion = s32[8,128,1]{2,0,1:T(8,128)S(1)} fusion(pred[8,128,1]{2,0,1:T(8,128)(4,1)S(1)} %copy.16, s32[8,128,1]{2,0,1:T(8,128)S(1)} %copy.15), kind=kOutput, calls=%fused_computation.12 | output fusion | flops 135168 | bytes 9216 | tf_op jit(solution)/shard_map/jit(cumsum)/reduce_window_sum | solution.py:48
  54.0 0.2 copy.17
  54.2 0.8 multiply_reduce_fusion
  54.9 0.1 copy.23
  55.0 0.7 and_reduce_fusion
  55.8 0.1 copy.22
  55.9 4.3 %scatter_custom_fusion.4 = s32[128]{0:T(128)S(1)} fusion(s32[1024]{0:T(1024)S(1)} %bitcast.49, s32[1024]{0:T(1024)S(1)} %fusion.6, s32[]{:T(128)} %constant.70.clone.1), kind=kCustom, calls=%fused_computation.72 | custom fusion | bytes 516
  60.4 4.3 %scatter_custom_fusion.3 = pred[128]{0:T(512)(128)(4,1)S(1)} fusion(s32[1024]{0:T(1024)S(1)} %bitcast.50, pred[1024]{0:T(1024)(128)(4,1)S(1)} %broadcast.224, pred[]{:T(512)} %constant.71.clone.1), kind=kCustom, calls=%fused_computation.62 | custom fusion | bytes 129
  64.8 6.6 %gather_fusion = bf16[128,3584]{1,0:T(8,128)(2,1)S(1)} fusion(bf16[1188,3584]{1,0:T(8,128)(2,1)} %param.6, s32[1024]{0:T(1024)S(1)} %pad_clamp_fusion.2), kind=kCustom, calls=%fused_computation.2 | custom fusion | bytes 1835520 | tf_op jit(solution)/shard_map/jit(_take)/gather | solution.py:57
  71.4 1.1 select_select_fusion
  72.5 3.7 %all-to-all-start = ((bf16[8,16,3584]{2,1,0:T(8,128)(2,1)}), bf16[8,16,3584]{2,1,0:T(8,128)(2,1)S(1)}, u32[]{:S(2)}, u32[]{:S(2)}) async-start(bf16[8,16,3584]{2,1,0:T(8,128)(2,1)} %select_select_fusion), calls=%async_computation | async-start | bytes 1835008 | tf_op jit(solution)/shard_map/all_to_all | solution.py:59
  76.4 0.2 reduce_window_sum.23
  76.6 0.2 select_reduce_fusion
  76.8 6.4 %scatter_fusion.1 = s32[8,16]{1,0:T(8,128)S(1)} fusion(s32[8,16]{1,0:T(8,128)S(1)} %broadcast.169, s32[128]{0:T(128)S(1)} %fusion.18, s32[128]{0:T(128)S(1)} %iota.14), kind=kCustom, calls=%fused_computation.4 | custom fusion | bytes 2560 | tf_op jit(solution)/shard_map/scatter | solution.py:76
  83.3 6.5 %scatter_fusion = pred[8,16]{1,0:T(8,128)(4,1)S(1)} fusion(pred[8,16]{1,0:T(8,128)(4,1)S(1)} %broadcast.166, s32[128]{0:T(128)S(1)} %fusion.18, pred[128]{0:T(512)(128)(4,1)S(1)} %broadcast.225), kind=kCustom, calls=%fused_computation.3 | custom fusion | bytes 1408 | tf_op jit(solution)/shard_map/scatter | solution.py:78
  89.9 1.6 %collective-permute-start.1 = (bf16[2,128,896]{2,1,0:T(8,128)(2,1)S(1)}, bf16[2,128,896]{2,1,0:T(8,128)(2,1)S(1)}, u32[]{:S(2)}, u32[]{:S(2)}) collective-permute-start(bf16[2,128,896]{2,1,0:T(8,128)(2,1)S(1)} %pad_maximum_fusion), channel_id=1, source_target_pairs={{0,16},{8,24},{16,0},{24,8},{1,17},{9,25},{17,1},{25,9},{2,18},{10... | collective-permute-start | bytes 1376264 | tf_op jit(solution)/shard_map/ppermute | solution.py:22
  91.5 7.6 %collective-permute-done.1 = bf16[2,128,896]{2,1,0:T(8,128)(2,1)S(1)} collective-permute-done((bf16[2,128,896]{2,1,0:T(8,128)(2,1)S(1)}, bf16[2,128,896]{2,1,0:T(8,128)(2,1)S(1)}, u32[]{:S(2)}, u32[]{:S(2)}) %collective-permute-start.1) | collective-permute-done | bytes 458784 | tf_op jit(solution)/shard_map/ppermute | solution.py:22
  99.4 1.1 gather_fusion.2
  100.5 0.2 broadcast_select_fusion
  100.7 1.1 broadcast_select_fusion.1
  101.8 5.4 %all-to-all-start.1 = ((bf16[8,16,3584]{2,1,0:T(8,128)(2,1)}), bf16[8,16,3584]{2,1,0:T(8,128)(2,1)S(1)}, u32[]{:S(2)}, u32[]{:S(2)}) async-start(bf16[8,16,3584]{2,1,0:T(8,128)(2,1)} %broadcast_select_fusion.1), calls=%async_computation.1 | async-start | bytes 1835008 | tf_op jit(solution)/shard_map/all_to_all | solution.py:84
  107.3 1.1 gather_fusion.1
  108.4 1.3 select_convert_fusion
  109.8 16.3 %all-to-all-done.1 = bf16[8,16,3584]{2,1,0:T(8,128)(2,1)S(1)} async-done(((bf16[8,16,3584]{2,1,0:T(8,128)(2,1)}), bf16[8,16,3584]{2,1,0:T(8,128)(2,1)S(1)}, u32[]{:S(2)}, u32[]{:S(2)}) %all-to-all-start.1) | async-done | bytes 917536 | tf_op jit(solution)/shard_map/all_to_all | solution.py:84
  126.1 10.0 %scatter_custom_fusion.2 = f32[1188,3584]{1,0:T(8,128)} fusion(s32[128]{0:T(128)S(1)} %fusion.16, f32[]{:T(128)} %constant.122.clone.1, bf16[128,3584]{1,0:T(8,128)(2,1)S(1)} %bitcast.43), kind=kCustom, calls=%fused_computation.8 | custom fusion | flops 917504 | bytes 17948676 | tf_op jit(solution)/shard_map/scatter-add | solution.py:89
  136.1 9.3 %convert_element_type.32 = bf16[1188,3584]{1,0:T(8,128)(2,1)} convert(f32[1188,3584]{1,0:T(8,128)} %scatter_custom_fusion.2) | non-fusion elementwise | flops 4257792 | bytes 25546752 | tf_op jit(solution)/shard_map/convert_element_type | solution.py:92
  145.3 2.8 %all-reduce.2.cloned.1.call-done = bf16[128,3584]{1,0:T(8,128)(2,1)} async-done(((bf16[128,3584]{1,0:T(8,128)(2,1)}), bf16[128,3584]{1,0:T(8,128)(2,1)}) %all-reduce.2.cloned.1.call-update) | async-done | bytes 917520 | tf_op jit(solution)/shard_map/psum | solution.py:91
  148.1 2.2 %copy.28 = bf16[128,3584]{1,0:T(8,128)(2,1)} copy(bf16[128,3584]{1,0:T(8,128)(2,1)} %all-reduce.2.cloned.1.call-done) | data formatting | bytes 1835008
  (42 shorter events, 1.1 us)
Async XLA Ops:
  7.2 69.1 %copy-start.1 = (s32[128]{0:T(128)S(1)}, s32[128]{0:T(128)}, u32[]{:S(2)}) copy-start(s32[128]{0:T(128)} %param.5) | copy-start | bytes 1540
  7.2 82.6 %collective-permute-start = (bf16[1,128,896]{2,1,0:T(8,128)(2,1)}, bf16[1,128,896]{2,1,0:T(8,128)(2,1)S(1)}, u32[]{:S(2)}, u32[]{:S(2)}) collective-permute-start(bf16[1,128,896]{2,1,0:T(8,128)(2,1)} %bitcast.44), channel_id=1, source_target_pairs={{0,8},{8,0},{16,24},{24,16},{1,9},{9,1},{17,25},{25,17},{2,10},{10... | collective-permute-start | bytes 688136 | tf_op jit(solution)/shard_map/ppermute | solution.py:22
  29.7 60.0 %copy-start = (bf16[128,896]{1,0:T(8,128)(2,1)S(1)}, bf16[128,896]{1,0:T(8,128)(2,1)}, u32[]{:S(2)}) copy-start(bf16[128,896]{1,0:T(8,128)(2,1)} %param.7) | copy-start | bytes 688132
  72.5 29.2 %all-to-all-start = ((bf16[8,16,3584]{2,1,0:T(8,128)(2,1)}), bf16[8,16,3584]{2,1,0:T(8,128)(2,1)S(1)}, u32[]{:S(2)}, u32[]{:S(2)}) async-start(bf16[8,16,3584]{2,1,0:T(8,128)(2,1)} %select_select_fusion), calls=%async_computation | async-start | bytes 1835008 | tf_op jit(solution)/shard_map/all_to_all | solution.py:59
  89.9 9.2 %collective-permute-start.1 = (bf16[2,128,896]{2,1,0:T(8,128)(2,1)S(1)}, bf16[2,128,896]{2,1,0:T(8,128)(2,1)S(1)}, u32[]{:S(2)}, u32[]{:S(2)}) collective-permute-start(bf16[2,128,896]{2,1,0:T(8,128)(2,1)S(1)} %pad_maximum_fusion), channel_id=1, source_target_pairs={{0,16},{8,24},{16,0},{24,8},{1,17},{9,25},{17,1},{25,9},{2,18},{10... | collective-permute-start | bytes 1376264 | tf_op jit(solution)/shard_map/ppermute | solution.py:22
  101.8 24.4 %all-to-all-start.1 = ((bf16[8,16,3584]{2,1,0:T(8,128)(2,1)}), bf16[8,16,3584]{2,1,0:T(8,128)(2,1)S(1)}, u32[]{:S(2)}, u32[]{:S(2)}) async-start(bf16[8,16,3584]{2,1,0:T(8,128)(2,1)} %broadcast_select_fusion.1), calls=%async_computation.1 | async-start | bytes 1835008 | tf_op jit(solution)/shard_map/all_to_all | solution.py:84
  107.2 40.9 %all-reduce.2.cloned.1.call-start = ((), (), s32[]{:S(2)}) async-start(), calls=%async_computation.2 | async-start | bytes 1835008 | tf_op jit(solution)/shard_map/psum | solution.py:91
Sparse Core Ops, SparseCore 0:
  111.0 37.1 all-reduce.1
